TPU v7x, 128 devices: a whole 4x4x4 slice. The times are simulated.
128 devices in a mesh: row: 32 (over y, x, core), col: 4 (over z).
Axes of the slice: x: 4, y: 4, z: 4, core: 2. Of those that a mesh axis runs over, the one named last changes fastest.
Arguments:
- stiff_bb: bfloat16 [384, 3, 128, 384], P(('row', 'col')), may hold values from -6 to 6
- stiff_bi: bfloat16 [384, 384, 3072], P(('row', 'col')), may hold values from -6 to 6
- constraint_modes: bfloat16 [384, 3072, 384], P(('row', 'col')), may hold values from -0.109375 to 0.109375
- interior_mass: float32 [384, 3072], P(('row', 'col')), may hold values from 0.25 to 4
- fixed_modes: bfloat16 [384, 3072, 256], P(('row', 'col')), may hold values from -6 to 6
- mass_bb: bfloat16 [384, 3, 128, 384], P(('row', 'col')), may hold values from -6 to 6
- boundary_map: int32 [384, 3], P(('row', 'col')), may hold values from 0 to 767, as said below
Outputs:
- interface_stiffness: float32 [768, 4, 128, 128], P('row', None, 'col')
- interface_mass: float32 [768, 4, 128, 128], P('row', None, 'col')
- mass_coupling: float32 [384, 256, 384], P(('row', 'col'))
Inputs may be any that keep to these rules, and one draw needn't show every extreme that they name: `boundary_map`: row s holds blocks b, b + a, b + c with 0 < a < c < 4, all three in the range of one owner (block // 24). Rows come in aligned row groups of 12; no owner serves more than 1 row of one row group, and in every draw one owner serves exactly 1 row of every row group.
All inputs are finite; a program needn't handle non-finite values.
Results may differ from a plain program's by a relative error of at most 0.0029.
Values sent between devices are 32-bit elements; how exact they have to be, the bound alone decides.
A program may use at most 192 MiB of HBM per device.

v0:
```python
import jax
import jax.numpy as jnp
from jax import lax
from jax.sharding import PartitionSpec as P

BAND = 4
BPO = 24


PAIRS = ((0, 0), (1, 1), (2, 2), (0, 1), (0, 2), (1, 2))


def owner_slots(mapping, slots_each):
    owner = mapping[:, 0] // BPO
    places = jnp.arange(owner.shape[0])
    earlier = (owner[:, None] == owner[None, :]) & (places[:, None] > places[None, :])
    return owner * slots_each + jnp.sum(earlier.astype(jnp.int32), axis=1)


def place_blocks(got_map, received, starting_owner):
    limit = BPO * BAND
    targets = []
    for first, second in PAIRS:
        rows = got_map[:, first]
        local = (rows - starting_owner) * BAND + got_map[:, second] - rows
        targets.append(jnp.where(rows >= 0, local, limit))
    flat = jnp.stack(targets, axis=1).reshape(-1)
    values = received.reshape((flat.shape[0],) + received.shape[2:])
    empty = jnp.zeros((limit,) + received.shape[2:], jnp.float32)
    return empty.at[flat].add(values, mode="drop")


def per_device(
    stiff_bb, stiff_bi, constraint_modes, interior_mass, fixed_modes, mass_bb, boundary_map
):
    owners = lax.axis_size("row")
    lanes = lax.axis_size("col")
    starting_owner = lax.axis_index("row") * BPO
    count = stiff_bi.shape[0]
    order = stiff_bi.shape[1]
    width = order // 3
    rows_per_portion = width // lanes
    slots_each = (count * lanes + owners - 1) // owners
    weighted = (interior_mass[:, :, None] * constraint_modes.astype(jnp.float32)).astype(
        jnp.bfloat16
    )
    red_k = stiff_bb.reshape(count, order, order).astype(jnp.float32) + jnp.einsum(
        "sbi,sic->sbc", stiff_bi, constraint_modes, preferred_element_type=jnp.float32
    )
    red_m = mass_bb.reshape(count, order, order).astype(jnp.float32) + jnp.einsum(
        "sib,sic->sbc", constraint_modes, weighted, preferred_element_type=jnp.float32
    )
    coupling = jnp.einsum("sim,sic->smc", fixed_modes, weighted, preferred_element_type=jnp.float32)
    reduced = jnp.stack([red_k, red_m], axis=1)
    pieces = [
        reduced[:, :, first * width : (first + 1) * width, second * width : (second + 1) * width]
        for first, second in PAIRS
    ]
    packets = jnp.stack(pieces, axis=1).reshape(count, 6, 2, lanes, rows_per_portion, width)
    packets = jnp.moveaxis(packets, 3, 0)
    tiled_map = jnp.broadcast_to(boundary_map[None], (lanes, count, 3))
    grouped, group_map = (
        lax.all_to_all(packets, "col", split_axis=0, concat_axis=1, tiled=True),
        lax.all_to_all(tiled_map, "col", split_axis=0, concat_axis=1, tiled=True),
    )
    grouped = grouped.reshape((lanes * count, 6, 2, rows_per_portion, width))
    group_map = group_map.reshape(lanes * count, 3)
    slot = owner_slots(group_map, slots_each)
    outgoing = (
        jnp.zeros((owners * slots_each, 6, 2, rows_per_portion, width), jnp.float32)
        .at[slot]
        .set(grouped)
    )
    out_map = jnp.full((owners * slots_each, 3), -1, jnp.int32).at[slot].set(group_map)
    received, got_map = (
        lax.all_to_all(outgoing, "row", split_axis=0, concat_axis=0, tiled=True),
        lax.all_to_all(out_map, "row", split_axis=0, concat_axis=0, tiled=True),
    )
    band = place_blocks(got_map, received, starting_owner).reshape(
        BPO, BAND, 2, rows_per_portion, width
    )
    return (band[:, :, 0], band[:, :, 1], coupling)


def solution(mesh):
    placed = (
        P(("row", "col"), None, None, None),
        P(("row", "col"), None, None),
        P(("row", "col"), None, None),
        P(("row", "col"), None),
        P(("row", "col"), None, None),
        P(("row", "col"), None, None, None),
        P(("row", "col"), None),
    )
    return jax.shard_map(
        per_device,
        mesh=mesh,
        in_specs=placed,
        out_specs=(
            P("row", None, "col", None),
            P("row", None, "col", None),
            P(("row", "col"), None, None),
        ),
        check_vma=False,
    )
```

profile of v0, /device:TPU:0, one launch (start us, length us, event | category | flops | bytes accessed | tf_op | source)
XLA Modules:
  0.0 185.7 jit_solution(3256829055502061644)
XLA Ops:
  0.6 0.8 copy.47
  1.4 0.6 broadcast_in_dim.34
  2.0 5.4 %all-to-all-start = ((s32[4,3,3]{1,2,0:T(4,128)}), s32[4,3,3]{1,2,0:T(4,128)S(1)}, u32[]{:S(2)}, u32[]{:S(2)}) async-start(s32[4,3,3]{1,2,0:T(4,128)} %broadcast_in_dim.34), calls=%async_computation | async-start | bytes 16384 | tf_op jit(solution)/shard_map/all_to_all | solution.py:64
  7.4 0.0 copy-start
  7.4 10.0 %fusion.4 = f32[3,1,384,384]{3,2,0,1:T(8,128)S(1)} fusion(bf16[3,384,384]{2,1,0:T(8,128)(2,1)} %bitcast.66, bf16[3,3072,384]{2,1,0:T(8,128)(2,1)} %param.9, f32[3,3072]{1,0:T(4,128)} %param.10), kind=kOutput, calls=%fused_computation.10 | convolution fusion | flops 2729410560 | bytes 9768960 | tf_op jit(solution)/shard_map/sib,sic->sbc/dot_general | solution.py:50
  17.4 0.0 copy-done
  17.4 8.2 %fusion.5 = f32[3,1,384,384]{3,2,0,1:T(8,128)S(1)} fusion(bf16[3,384,384]{2,1,0:T(8,128)(2,1)S(1)} %bitcast.67, bf16[3,384,3072]{2,1,0:T(8,128)(2,1)} %param.8, bf16[3,3072,384]{2,1,0:T(8,128)(2,1)} %param.9), kind=kOutput, calls=%fused_computation.12 | convolution fusion | flops 2718793728 | bytes 16809984 | tf_op jit(solution)/shard_map/sbi,sic->sbc/dot_general | solution.py:47
  25.7 0.3 pad_maximum_fusion
  26.2 1.7 copy.73
  27.9 0.0 all-to-all-done
  27.9 4.8 %all-to-all-start.2 = ((f32[4,3,6,2,32,128]{5,4,3,2,1,0:T(8,128)}), f32[4,3,6,2,32,128]{5,4,3,2,1,0:T(8,128)S(1)}, u32[]{:S(2)}, u32[]{:S(2)}) async-start(f32[4,3,6,2,32,128]{5,4,3,2,1,0:T(8,128)} %bitcast.57), calls=%async_computation.2 | async-start | bytes 4718592 | tf_op jit(solution)/shard_map/all_to_all | solution.py:63
  32.6 0.1 reshape.120
  32.7 0.1 copy.49
  32.9 0.2 convert_reduce_fusion
  33.1 1.2 scatter_custom_fusion
  34.2 27.0 %all-to-all-done.2 = f32[4,3,6,2,32,128]{5,4,3,2,1,0:T(8,128)S(1)} async-done(((f32[4,3,6,2,32,128]{5,4,3,2,1,0:T(8,128)}), f32[4,3,6,2,32,128]{5,4,3,2,1,0:T(8,128)S(1)}, u32[]{:S(2)}, u32[]{:S(2)}) %all-to-all-start.2) | async-done | bytes 2359328 | tf_op jit(solution)/shard_map/all_to_all | solution.py:63
  61.3 7.3 %all-to-all-start.1 = ((s32[32,1,3]{2,1,0:T(1,128)}), s32[32,1,3]{2,1,0:T(1,128)S(1)}, u32[]{:S(2)}, u32[]{:S(2)}) async-start(s32[32,1,3]{2,1,0:T(1,128)} %bitcast.26), calls=%async_computation.1 | async-start | bytes 32768 | tf_op jit(solution)/shard_map/all_to_all | solution.py:77
  68.6 3.5 %broadcast_in_dim.36 = f32[32,6,2,32,128]{4,3,2,1,0:T(8,128)} broadcast(f32[]{:T(128)} %constant.10.clone.1), dimensions={} | broadcast | bytes 6291460 | tf_op jit(solution)/shard_map/broadcast_in_dim | solution.py:70
  72.0 5.7 %scatter_fusion = f32[32,6,2,32,128]{4,3,2,1,0:T(8,128)} fusion(f32[32,6,2,32,128]{4,3,2,1,0:T(8,128)} %broadcast_in_dim.36, s32[12]{0:T(128)S(1)} %fusion.10, f32[12,6,2,32,128]{4,3,2,1,0:T(8,128)S(1)} %bitcast.56), kind=kCustom, calls=%fused_computation.1 | custom fusion | bytes 7077936 | tf_op jit(solution)/shard_map/scatter | solution.py:72
  77.7 0.0 copy-start.1
  77.7 0.0 all-to-all-done.1
  77.7 7.8 %all-to-all-start.3 = ((f32[32,6,2,32,128]{4,3,2,1,0:T(8,128)}), f32[32,6,2,32,128]{4,3,2,1,0:T(8,128)}, u32[]{:S(2)}, u32[]{:S(2)}) async-start(f32[32,6,2,32,128]{4,3,2,1,0:T(8,128)} %scatter_fusion), calls=%async_computation.3 | async-start | bytes 12582912 | tf_op jit(solution)/shard_map/all_to_all | solution.py:76
  85.6 0.0 copy-done.1
  85.6 8.5 %fusion.6 = f32[3,256,384]{1,2,0:T(8,128)S(1)} fusion(bf16[3,3072,256]{2,1,0:T(8,128)(2,1)} %param.11, bf16[3,3072,384]{2,1,0:T(8,128)(2,1)} %param.9, f32[3,3072]{1,0:T(4,128)S(1)} %copy-done.1), kind=kOutput, calls=%fused_computation.15 | convolution fusion | flops 1822556160 | bytes 13012992 | tf_op jit(solution)/shard_map/sim,sic->smc/dot_general | solution.py:53
  94.1 1.4 copy.64
  95.5 0.1 copy.52
  95.6 0.1 copy.53
  95.7 0.1 reshape.110
  95.8 67.4 %all-to-all-done.3 = f32[32,6,2,32,128]{4,3,2,1,0:T(8,128)} async-done(((f32[32,6,2,32,128]{4,3,2,1,0:T(8,128)}), f32[32,6,2,32,128]{4,3,2,1,0:T(8,128)}, u32[]{:S(2)}, u32[]{:S(2)}) %all-to-all-start.3) | async-done | bytes 6291488 | tf_op jit(solution)/shard_map/all_to_all | solution.py:76
  163.3 0.4 broadcast_in_dim.32
  163.7 20.0 %scatter_fusion.1 = f32[96,2,32,128]{3,2,1,0:T(8,128)S(1)} fusion(f32[96,2,32,128]{3,2,1,0:T(8,128)S(1)} %broadcast_in_dim.32, s32[192]{0:T(256)S(1)} %bitcast.65, f32[192,2,32,128]{3,2,1,0:T(8,128)} %bitcast.21), kind=kCustom, calls=%fused_computation.2 | custom fusion | flops 1572864 | bytes 18875136 | tf_op jit(solution)/shard_map/scatter-add | solution.py:30
  183.6 2.0 %slice_bitcast_fusion = (f32[24,4,32,128]{3,2,1,0:T(8,128)}, f32[24,4,32,128]{3,2,1,0:T(8,128)}) fusion(f32[24,4,2,32,128]{4,3,2,1,0:T(8,128)S(1)} %bitcast.55), kind=kLoop, calls=%fused_computation.13 | loop fusion | bytes 6291456 | tf_op jit(solution)/shard_map/squeeze | solution.py:82
  (13 shorter events, 0.3 us)
Async XLA Ops:
  2.0 25.9 %all-to-all-start = ((s32[4,3,3]{1,2,0:T(4,128)}), s32[4,3,3]{1,2,0:T(4,128)S(1)}, u32[]{:S(2)}, u32[]{:S(2)}) async-start(s32[4,3,3]{1,2,0:T(4,128)} %broadcast_in_dim.34), calls=%async_computation | async-start | bytes 16384 | tf_op jit(solution)/shard_map/all_to_all | solution.py:64
  7.4 10.0 %copy-start = (bf16[3,3,128,384]{3,2,1,0:T(8,128)(2,1)S(1)}, bf16[3,3,128,384]{3,2,1,0:T(8,128)(2,1)}, u32[]{:S(2)}) copy-start(bf16[3,3,128,384]{3,2,1,0:T(8,128)(2,1)} %param.7) | copy-start | bytes 2654212
  27.9 33.4 %all-to-all-start.2 = ((f32[4,3,6,2,32,128]{5,4,3,2,1,0:T(8,128)}), f32[4,3,6,2,32,128]{5,4,3,2,1,0:T(8,128)S(1)}, u32[]{:S(2)}, u32[]{:S(2)}) async-start(f32[4,3,6,2,32,128]{5,4,3,2,1,0:T(8,128)} %bitcast.57), calls=%async_computation.2 | async-start | bytes 4718592 | tf_op jit(solution)/shard_map/all_to_all | solution.py:63
  61.3 16.5 %all-to-all-start.1 = ((s32[32,1,3]{2,1,0:T(1,128)}), s32[32,1,3]{2,1,0:T(1,128)S(1)}, u32[]{:S(2)}, u32[]{:S(2)}) async-start(s32[32,1,3]{2,1,0:T(1,128)} %bitcast.26), calls=%async_computation.1 | async-start | bytes 32768 | tf_op jit(solution)/shard_map/all_to_all | solution.py:77
  77.7 7.9 %copy-start.1 = (f32[3,3072]{1,0:T(4,128)S(1)}, f32[3,3072]{1,0:T(4,128)}, u32[]{:S(2)}) copy-start(f32[3,3072]{1,0:T(4,128)} %param.10) | copy-start | bytes 110596
  77.7 85.6 %all-to-all-start.3 = ((f32[32,6,2,32,128]{4,3,2,1,0:T(8,128)}), f32[32,6,2,32,128]{4,3,2,1,0:T(8,128)}, u32[]{:S(2)}, u32[]{:S(2)}) async-start(f32[32,6,2,32,128]{4,3,2,1,0:T(8,128)} %scatter_fusion), calls=%async_computation.3 | async-start | bytes 12582912 | tf_op jit(solution)/shard_map/all_to_all | solution.py:76
where the time goes:
time: 187 us; the launch traced here: 186 us
  waiting for transfers between devices  94.5 us (51%)
  matrix products  26.7 us (14%)
  starting transfers between devices  25.3 us (14%)
  other arithmetic  20.5 us (11%)
  local copies, waits for them, and re-layouts  17.8 us (10%)
    all_to_all x1, waiting for transfers between devices, per_device(): lax.all_to_all(outgoing, 'row', split_axis=0, concat_axis=0, tiled=True)  67.4 us
    all_to_all x1, waiting for transfers between devices, per_device(): lax.all_to_all(packets, 'col', split_axis=0, concat_axis=1, tiled=True)  27 us
    scatter-add x1, other arithmetic, place_blocks(): return empty.at[flat].add(values, mode='drop')  20 us
    dot_general x1, matrix products, per_device(): jnp.einsum('sib,sic->sbc', constraint_modes, weighted, preferred_element_...  10 us
    dot_general x1, matrix products, per_device(): jnp.einsum('sim,sic->smc', fixed_modes, weighted, preferred_element_type=...  8.54 us
    dot_general x1, matrix products, per_device(): jnp.einsum('sbi,sic->sbc', stiff_bi, constraint_modes, preferred_element_...  8.2 us
    all_to_all x1, starting transfers between devices, per_device(): lax.all_to_all(outgoing, 'row', split_axis=0, concat_axis=0, tiled=True)  7.83 us
    all_to_all x1, starting transfers between devices, per_device(): lax.all_to_all(out_map, 'row', split_axis=0, concat_axis=0, tiled=True)  7.31 us
  transfers between devices with their start and end apart: 4, of which 2 were waited for; matrix products, arithmetic and copies ran while one was open for 22% of the time, Pallas kernels for 0%

commit v1 on v0

v1 whole, which is shorter than its diff:
```python
import functools

import jax
import jax.numpy as jnp
from jax import lax
from jax.experimental import pallas as pl
from jax.experimental.pallas import tpu as pltpu
from jax.sharding import PartitionSpec as P

BAND = 4
BPO = 24
MESH = pl.DeviceIdType.MESH

PAIRS = ((2, 2), (1, 1), (1, 2), (0, 0), (0, 1), (0, 2))
CHUNKS = ((0, 2, 0, 1), (0, 1, 1, 2), (0, 0, 3, 3), (1, 0, 9, 3), (1, 1, 7, 2), (1, 2, 6, 1))


def ring_place(me, t):
    y, x, k = me // 8, (me // 2) % 4, me % 2
    dx = t % 4
    dy = (t // 4 + t) % 4
    dk = t // 16
    return ((y + dy) % 4) * 8 + ((x + dx) % 4) * 2 + (k + dk) % 2


def reduce_and_send(
    owners, lanes,
    map_ref, mass_ref, sbb_hbm, sbi_hbm, psi_hbm, fix_hbm, mbb_hbm,
    recv_hbm, table_ref, coup_hbm,
    psi, sbi, fix, wgt, sbb, mbb, msq, coup, zmap, zmap_s, rmap, rmap_s, pick,
    r0, r1, r2, r3, r4, r5, z0, z1, z2, z3, z4, z5, s0, s1, s2, s3, s4, s5,
    in_sem, coup_sem, zm_send, zm_recv, zm_loc, rm_send, rm_recv, rm_loc,
    z_send, z_recv, x_send, x_recv, x_own,
):
    reds, zs, slots = (r0, r1, r2, r3, r4, r5), (z0, z1, z2, z3, z4, z5), (s0, s1, s2, s3, s4, s5)
    me, lane = lax.axis_index("row"), lax.axis_index("col")
    count, order = psi.shape[0], psi.shape[2]
    width = order // 3
    part = width // lanes

    loads = {}

    def load(name, src, dst, sem):
        loads[name] = pltpu.make_async_copy(src, dst, in_sem.at[sem])
        loads[name].start()

    for i, b in enumerate((2, 1, 0)):
        cols = pl.ds(b * width, width)
        load(("psi", b), psi_hbm.at[:, :, cols], psi.at[:, :, cols], 2 * i)
        load(("sbi", b), sbi_hbm.at[:, cols, :], sbi.at[:, cols, :], 2 * i + 1)
        if i == 0:
            load("sbb", sbb_hbm, sbb, 6)
    load("mbb", mbb_hbm, mbb, 7)
    load("fix", fix_hbm, fix, 8)

    barrier = pltpu.get_barrier_semaphore()
    for d in range(1, lanes):
        pl.semaphore_signal(barrier, inc=1, device_id=(me, lax.rem(lane + d, lanes)), device_id_type=MESH)

    def greet(t, carry):
        pl.semaphore_signal(barrier, inc=1, device_id=(ring_place(me, t), lane), device_id_type=MESH)
        return carry

    lax.fori_loop(1, owners, greet, 0)
    pl.semaphore_wait(barrier, owners + lanes - 2)

    zmap[pl.ds(lane, 1)] = map_ref[...]
    map_sends = []
    for d in range(1, lanes):
        peer = lax.rem(lane + d, lanes)
        copy = pltpu.make_async_remote_copy(
            src_ref=map_ref, dst_ref=zmap.at[pl.ds(lane, 1)], send_sem=zm_send.at[d - 1],
            recv_sem=zm_recv.at[d - 1], device_id=(me, peer), device_id_type=MESH)
        copy.start()
        map_sends.append(copy)

    def stiff_block(b, red):
        n = 3 - b

        def one(s, carry):
            out = jnp.dot(sbi[s, pl.ds(b * width, width), :], psi[s, :, pl.ds(b * width, n * width)],
                          preferred_element_type=jnp.float32)
            out = out + sbb[s, b, :, pl.ds(b * width, n * width)].astype(jnp.float32)
            for q in range(n):
                red[s, q] = out[:, q * width:(q + 1) * width]
            return carry

        lax.fori_loop(0, count, one, 0)

    def mass_block(b, red):
        n = 3 - b

        def one(s, carry):
            out = lax.dot_general(psi[s, :, pl.ds(b * width, width)], wgt[s, :, pl.ds(b * width, n * width)],
                                  (((0,), (0,)), ((), ())), preferred_element_type=jnp.float32)
            out = out + mbb[s, b, :, pl.ds(b * width, n * width)].astype(jnp.float32)
            for q in range(n):
                red[s, q] = out[:, q * width:(q + 1) * width]
            return carry

        lax.fori_loop(0, count, one, 0)

    z_copies = {}

    def send_lanes(c):
        red, z = reds[c], zs[c]
        z[pl.ds(count * lane, count)] = red[:, :, pl.ds(pl.multiple_of(part * lane, part), part), :]
        for d in range(1, lanes):
            peer = lax.rem(lane + d, lanes)
            copy = pltpu.make_async_remote_copy(
                src_ref=red.at[:, :, pl.ds(pl.multiple_of(part * peer, part), part), :],
                dst_ref=z.at[pl.ds(count * lane, count)], send_sem=z_send.at[c, d - 1],
                recv_sem=z_recv.at[c, d - 1], device_id=(me, peer), device_id_type=MESH)
            copy.start()
            z_copies[c, d] = copy

    def send_owners(c):
        z, slot = zs[c], slots[c]
        first, n = CHUNKS[c][2], CHUNKS[c][3]
        for d in range(1, lanes):
            z_copies[c, d].wait_recv()

        def one(t, carry):
            to = ring_place(me, t)
            slot[t] = z[pick[to]]
            pltpu.make_async_remote_copy(
                src_ref=slot.at[t], dst_ref=recv_hbm.at[me, pl.ds(first, n)], send_sem=x_send.at[c],
                recv_sem=x_recv.at[c], device_id=(to, lane), device_id_type=MESH).start()
            return carry

        lax.fori_loop(1, owners, one, 0)
        slot[0] = z[pick[me]]
        pltpu.make_async_copy(slot.at[0], recv_hbm.at[me, pl.ds(first, n)], x_own.at[c]).start()

    loads["psi", 2].wait()
    loads["sbi", 2].wait()
    loads["sbb"].wait()
    stiff_block(2, reds[0])
    send_lanes(0)
    loads["psi", 1].wait()
    loads["sbi", 1].wait()
    stiff_block(1, reds[1])
    send_lanes(1)

    for d in range(1, lanes):
        map_sends[d - 1].wait_recv()
    to_scalars = pltpu.make_async_copy(zmap, zmap_s, zm_loc)
    to_scalars.start()

    def tell(t, carry):
        pltpu.make_async_remote_copy(
            src_ref=zmap, dst_ref=rmap.at[me], send_sem=rm_send, recv_sem=rm_recv,
            device_id=(ring_place(me, t), lane), device_id_type=MESH).start()
        return carry

    lax.fori_loop(1, owners, tell, 0)
    rmap[me] = zmap[...]
    to_scalars.wait()
    heads = [zmap_s[j // count, 0, 3 * (j % count)] // BPO for j in range(lanes * count)]

    def choose(o, carry):
        found = jnp.int32(0)
        for j, head in enumerate(heads):
            found = jnp.where(head == o, jnp.int32(j), found)
        pick[o] = found
        return carry

    lax.fori_loop(0, owners, choose, 0)

    loads["psi", 0].wait()
    loads["sbi", 0].wait()
    stiff_block(0, reds[2])
    send_lanes(2)
    send_owners(0)

    blocks = psi.shape[1] // 128

    def weigh(s, carry):
        turned = msq[s].T
        for a in range(blocks):
            rows = slice(a * 128, (a + 1) * 128)
            wgt[s, rows, :] = (turned[:, a:a + 1] * psi[s, rows, :].astype(jnp.float32)).astype(jnp.bfloat16)
        return carry

    msq[...] = jnp.zeros_like(msq)
    for s in range(count):
        for a in range(blocks):
            msq[s, a:a + 1, :] = mass_ref[s:s + 1, a * 128:(a + 1) * 128]
    lax.fori_loop(0, count, weigh, 0)
    send_owners(1)

    loads["mbb"].wait()
    mass_block(0, reds[3])
    send_lanes(3)
    send_owners(2)
    mass_block(1, reds[4])
    send_lanes(4)
    mass_block(2, reds[5])
    send_lanes(5)
    send_owners(3)

    pltpu.make_async_copy(rmap.at[pl.ds(0, owners - 1)], rmap.at[pl.ds(0, owners - 1)], rm_recv).wait()
    to_scalars = pltpu.make_async_copy(rmap, rmap_s, rm_loc)
    to_scalars.start()
    to_scalars.wait()

    def place(r, carry):
        found = [jnp.int32(-1)] * 3
        for j in range(lanes * count):
            got = [rmap_s[r, j // count, 0, 3 * (j % count) + i] for i in range(3)]
            mine = got[0] // BPO == me
            found = [jnp.where(mine, g - me * BPO, f) for g, f in zip(got, found)]
        for i in range(3):
            table_ref[r, i] = found[i]
        return carry

    lax.fori_loop(0, owners, place, 0)

    loads["fix"].wait()

    def couple(s, carry):
        coup[s] = lax.dot_general(fix[s], wgt[s], (((0,), (0,)), ((), ())), preferred_element_type=jnp.float32)
        return carry

    lax.fori_loop(0, count, couple, 0)
    coup_copy = pltpu.make_async_copy(coup, coup_hbm, coup_sem)
    coup_copy.start()
    send_owners(4)
    send_owners(5)

    coup_copy.wait()
    for d in range(1, lanes):
        map_sends[d - 1].wait_send()
    pltpu.make_async_copy(rmap.at[pl.ds(0, owners - 1)], rmap.at[pl.ds(0, owners - 1)], rm_send).wait()
    for c, (_, _, first, n) in enumerate(CHUNKS):
        for d in range(1, lanes):
            z_copies[c, d].wait_send()
        pltpu.make_async_copy(slots[c].at[0], recv_hbm.at[me, pl.ds(first, n)], x_own.at[c]).wait()
        sent = slots[c].at[pl.ds(1, owners - 1)]
        pltpu.make_async_copy(sent, sent, x_send.at[c]).wait()
        pltpu.make_async_copy(sent, sent, x_recv.at[c]).wait()


def assemble(owners, table_ref, recv_hbm, k_ref, m_ref, buf, sem):
    def fetch(r):
        return pltpu.make_async_copy(recv_hbm.at[r], buf.at[r], sem.at[r])

    def begin(r, carry):
        @pl.when(table_ref[r, 0] >= 0)
        def _():
            fetch(r).start()

        return carry

    lax.fori_loop(0, owners, begin, 0)

    def clear(e, carry):
        k_ref[e] = jnp.zeros(k_ref.shape[1:], jnp.float32)
        m_ref[e] = jnp.zeros(m_ref.shape[1:], jnp.float32)
        return carry

    lax.fori_loop(0, BPO * BAND, clear, 0)

    def add(r, carry):
        @pl.when(table_ref[r, 0] >= 0)
        def _():
            places = [table_ref[r, i] for i in range(3)]
            fetch(r).wait()
            for p, (i, j) in enumerate(PAIRS):
                e = places[i] * BAND + places[j] - places[i]
                k_ref[e] += buf[r, p]
                m_ref[e] += buf[r, len(PAIRS) + p]

        return carry

    lax.fori_loop(0, owners, add, 0)


def per_device(stiff_bb, stiff_bi, constraint_modes, interior_mass, fixed_modes, mass_bb, boundary_map):
    owners, lanes = lax.axis_size("row"), lax.axis_size("col")
    count, inner, order = constraint_modes.shape
    modes = fixed_modes.shape[2]
    width = order // 3
    part = width // lanes
    planes = 2 * len(PAIRS)
    maps = jnp.pad(boundary_map.reshape(1, 1, 3 * count), ((0, 0), (0, 0), (0, 128 - 3 * count)))

    anywhere = pl.BlockSpec(memory_space=pl.ANY)
    in_vmem = pl.BlockSpec(memory_space=pltpu.VMEM)
    f32, bf16, i32 = jnp.float32, jnp.bfloat16, jnp.int32
    dma = pltpu.SemaphoreType.DMA
    received, table, coupling = pl.pallas_call(
        functools.partial(reduce_and_send, owners, lanes),
        out_shape=(
            jax.ShapeDtypeStruct((owners, planes, part, width), f32),
            jax.ShapeDtypeStruct((owners, 4), i32),
            jax.ShapeDtypeStruct((count, modes, order), f32),
        ),
        in_specs=[in_vmem, in_vmem] + [anywhere] * 5,
        out_specs=(anywhere, pl.BlockSpec(memory_space=pltpu.SMEM), anywhere),
        scratch_shapes=[
            pltpu.VMEM((count, inner, order), bf16),
            pltpu.VMEM((count, order, inner), bf16),
            pltpu.VMEM((count, inner, modes), bf16),
            pltpu.VMEM((count, inner, order), bf16),
            pltpu.VMEM((count, 3, width, order), bf16),
            pltpu.VMEM((count, 3, width, order), bf16),
            pltpu.VMEM((count, 128, 128), f32),
            pltpu.VMEM((count, modes, order), f32),
            pltpu.VMEM((lanes, 1, 128), i32),
            pltpu.SMEM((lanes, 1, 128), i32),
            pltpu.VMEM((owners, lanes, 1, 128), i32),
            pltpu.SMEM((owners, lanes, 1, 128), i32),
            pltpu.SMEM((owners,), i32),
        ]
        + [pltpu.VMEM((count, n, width, width), f32) for _, _, _, n in CHUNKS]
        + [pltpu.VMEM((count * lanes, n, part, width), f32) for _, _, _, n in CHUNKS]
        + [pltpu.VMEM((owners, n, part, width), f32) for _, _, _, n in CHUNKS]
        + [
            dma((9,)), dma, dma((lanes - 1,)), dma((lanes - 1,)), dma, dma, dma, dma,
            dma((len(CHUNKS), lanes - 1)), dma((len(CHUNKS), lanes - 1)),
            dma((len(CHUNKS),)), dma((len(CHUNKS),)), dma((len(CHUNKS),)),
        ],
        compiler_params=pltpu.CompilerParams(
            collective_id=0, has_side_effects=True, vmem_limit_bytes=60 * 1024 * 1024),
        name="reduce_and_send",
    )(maps, interior_mass, stiff_bb, stiff_bi, constraint_modes, fixed_modes, mass_bb)

    entry = jax.ShapeDtypeStruct((BPO * BAND, part, width), f32)
    k_band, m_band = pl.pallas_call(
        functools.partial(assemble, owners),
        out_shape=(entry, entry),
        in_specs=[pl.BlockSpec(memory_space=pltpu.SMEM), anywhere],
        out_specs=(in_vmem, in_vmem),
        scratch_shapes=[pltpu.VMEM((owners, planes, part, width), f32), dma((owners,))],
        compiler_params=pltpu.CompilerParams(vmem_limit_bytes=40 * 1024 * 1024),
        name="assemble",
    )(table, received)
    banded = (BPO, BAND, part, width)
    return k_band.reshape(banded), m_band.reshape(banded), coupling


def solution(mesh):
    both = ("row", "col")
    return jax.shard_map(
        per_device,
        mesh=mesh,
        in_specs=(
            P(both, None, None, None), P(both, None, None), P(both, None, None), P(both, None),
            P(both, None, None), P(both, None, None, None), P(both, None),
        ),
        out_specs=(P("row", None, "col", None), P("row", None, "col", None), P(both, None, None)),
        check_vma=False,
    )
```

time: 187 us -> 106 us (0.57)
  the two profiles are of different devices: /device:TPU:0 before, /device:TPU:1 now
where the time goes in v1:
time: 106 us; the launch traced here: 107 us
  Pallas kernels  100 us (94%)
  local copies, waits for them, and re-layouts  5.8 us (5%)
    pallas_call x1, Pallas kernels, per_device(): pl.pallas_call(functools.partial(reduce_and_send, owners, lanes), out_sha...  89.5 us
    pallas_call x1, Pallas kernels, per_device(): pl.pallas_call(functools.partial(assemble, owners), out_shape=(entry, ent...  10.7 us
    unnamed x7, local copies, waits for them, and re-layouts  4.51 us

profile of v1, /device:TPU:1, one launch (start us, length us, event | category | flops | bytes accessed | tf_op | source)
XLA Modules:
  0.0 106.7 jit_solution(11997724766548159117)
XLA Ops:
  0.6 0.8 reshape.15
  1.4 0.5 pad.4.map_ref
  1.9 89.5 %reduce_and_send.1 = (f32[32,12,32,128]{3,2,1,0:T(8,128)}, s32[32,4]{1,0:T(8,128)}, f32[3,256,384]{2,1,0:T(8,128)}) custom-call(s32[1,1,128]{2,1,0:T(1,128)} %pad.4.map_ref, f32[3,3072]{1,0:T(4,128)} %mass_ref.1, bf16[3,3,128,384]{3,2,1,0:T(8,128)(2,1)} %sbb_hbm.1, bf16[3,384,3072]{2,1,0:T(8,128)(2,1)} %sbi_hbm.1, bf16[3,3072,384]{2,1,0:T(8,128)(2,1)} %psi_hbm.1, ...), custom_call_target="tpu_custom_call" | custom-call | tf_op jit(solution)/shard_map/reduce_and_send/pallas_call | solution.py:292
  91.4 0.0 copy-start
  91.5 2.8 %copy-done = f32[32,12,32,128]{3,2,1,0:T(8,128)S(1)} copy-done((f32[32,12,32,128]{3,2,1,0:T(8,128)S(1)}, f32[32,12,32,128]{3,2,1,0:T(8,128)}, u32[]{:S(2)}) %copy-start) | copy-done | bytes 6291480
  94.2 0.0 copy-start.1
  94.2 0.7 copy-done.1
  94.9 0.0 copy-start.2
  94.9 10.7 %assemble.1 = (f32[96,32,128]{2,1,0:T(8,128)}, f32[96,32,128]{2,1,0:T(8,128)}) custom-call(s32[32,4]{1,0:T(8,128)S(1)} %copy-done.1, f32[32,12,32,128]{3,2,1,0:T(8,128)S(1)} %copy-done), custom_call_target="tpu_custom_call" | custom-call | tf_op jit(solution)/shard_map/assemble/pallas_call | solution.py:330
  105.7 0.0 copy-done.2
  105.7 1.0 copy.11
Async XLA Ops:
  91.4 2.8 %copy-start = (f32[32,12,32,128]{3,2,1,0:T(8,128)S(1)}, f32[32,12,32,128]{3,2,1,0:T(8,128)}, u32[]{:S(2)}) copy-start(f32[32,12,32,128]{3,2,1,0:T(8,128)} %get-tuple-element.9.recv_hbm) | copy-start | bytes 18874372
  94.2 0.7 copy-start.1
  94.9 10.8 %copy-start.2 = (f32[3,256,384]{2,1,0:T(8,128)S(1)}, f32[3,256,384]{2,1,0:T(8,128)}, u32[]{:S(2)}) copy-start(f32[3,256,384]{2,1,0:T(8,128)} %get-tuple-element.18) | copy-start | bytes 3538948

commit v2 on v1

--- a/solution.py
+++ b/solution.py
@@ -25,11 +25,11 @@
 
 def reduce_and_send(
     owners, lanes,
-    map_ref, mass_ref, sbb_hbm, sbi_hbm, psi_hbm, fix_hbm, mbb_hbm,
-    recv_hbm, table_ref, coup_hbm,
-    psi, sbi, fix, wgt, sbb, mbb, msq, coup, zmap, zmap_s, rmap, rmap_s, pick,
+    map_hbm, mass_hbm, sbb_hbm, sbi_hbm, psi_hbm, fix_hbm, mbb_hbm,
+    recv_hbm, table_hbm, coup_hbm,
+    psi, sbi, fix, wgt, sbb, mbb, mass, msq, coup, map_s, mine, zmap, zmap_s, rmap, rmap_s, pick, table,
     r0, r1, r2, r3, r4, r5, z0, z1, z2, z3, z4, z5, s0, s1, s2, s3, s4, s5,
-    in_sem, coup_sem, zm_send, zm_recv, zm_loc, rm_send, rm_recv, rm_loc,
+    in_sem, coup_sem, table_sem, zm_send, zm_recv, zm_loc, rm_send, rm_recv, rm_loc,
     z_send, z_recv, x_send, x_recv, x_own,
 ):
     reds, zs, slots = (r0, r1, r2, r3, r4, r5), (z0, z1, z2, z3, z4, z5), (s0, s1, s2, s3, s4, s5)
@@ -40,18 +40,22 @@
 
     loads = {}
 
-    def load(name, src, dst, sem):
-        loads[name] = pltpu.make_async_copy(src, dst, in_sem.at[sem])
+    def load(name, src, dst):
+        loads[name] = pltpu.make_async_copy(src, dst, in_sem.at[len(loads)])
         loads[name].start()
 
-    for i, b in enumerate((2, 1, 0)):
+    def load_block(b):
         cols = pl.ds(b * width, width)
-        load(("psi", b), psi_hbm.at[:, :, cols], psi.at[:, :, cols], 2 * i)
-        load(("sbi", b), sbi_hbm.at[:, cols, :], sbi.at[:, cols, :], 2 * i + 1)
-        if i == 0:
-            load("sbb", sbb_hbm, sbb, 6)
-    load("mbb", mbb_hbm, mbb, 7)
-    load("fix", fix_hbm, fix, 8)
+        load(("psi", b), psi_hbm.at[:, :, cols], psi.at[:, :, cols])
+        load(("sbi", b), sbi_hbm.at[:, cols, :], sbi.at[:, cols, :])
+        load(("sbb", b), sbb_hbm.at[:, b], sbb.at[:, b])
+
+    def loaded(b):
+        for name in ("psi", "sbi", "sbb"):
+            loads[name, b].wait()
+
+    load("map", map_hbm, map_s)
+    load_block(2)
 
     barrier = pltpu.get_barrier_semaphore()
     for d in range(1, lanes):
@@ -61,15 +65,25 @@
         pl.semaphore_signal(barrier, inc=1, device_id=(ring_place(me, t), lane), device_id_type=MESH)
         return carry
 
+    loads["map"].wait()
+    lanes_of = lax.broadcasted_iota(jnp.int32, (1, 1, 128), 2)
+
+    def as_row(scalars):
+        row = jnp.zeros((1, 1, 128), jnp.int32)
+        for i, scalar in enumerate(scalars):
+            row = jnp.where(lanes_of == i, scalar, row)
+        return row
+
+    own = as_row([map_s[s, i] for s in range(count) for i in range(3)])
+    mine[...] = own
+    zmap[pl.ds(lane, 1)] = own
     lax.fori_loop(1, owners, greet, 0)
     pl.semaphore_wait(barrier, owners + lanes - 2)
-
-    zmap[pl.ds(lane, 1)] = map_ref[...]
     map_sends = []
     for d in range(1, lanes):
         peer = lax.rem(lane + d, lanes)
         copy = pltpu.make_async_remote_copy(
-            src_ref=map_ref, dst_ref=zmap.at[pl.ds(lane, 1)], send_sem=zm_send.at[d - 1],
+            src_ref=mine, dst_ref=zmap.at[pl.ds(lane, 1)], send_sem=zm_send.at[d - 1],
             recv_sem=zm_recv.at[d - 1], device_id=(me, peer), device_id_type=MESH)
         copy.start()
         map_sends.append(copy)
@@ -132,13 +146,12 @@
         slot[0] = z[pick[me]]
         pltpu.make_async_copy(slot.at[0], recv_hbm.at[me, pl.ds(first, n)], x_own.at[c]).start()
 
-    loads["psi", 2].wait()
-    loads["sbi", 2].wait()
-    loads["sbb"].wait()
+    loaded(2)
+    load_block(1)
     stiff_block(2, reds[0])
     send_lanes(0)
-    loads["psi", 1].wait()
-    loads["sbi", 1].wait()
+    loaded(1)
+    load_block(0)
     stiff_block(1, reds[1])
     send_lanes(1)
 
@@ -167,8 +180,10 @@
 
     lax.fori_loop(0, owners, choose, 0)
 
-    loads["psi", 0].wait()
-    loads["sbi", 0].wait()
+    loaded(0)
+    load("mass", mass_hbm, mass)
+    load("mbb", mbb_hbm, mbb)
+    load("fix", fix_hbm, fix)
     stiff_block(0, reds[2])
     send_lanes(2)
     send_owners(0)
@@ -183,9 +198,10 @@
         return carry
 
     msq[...] = jnp.zeros_like(msq)
+    loads["mass"].wait()
     for s in range(count):
         for a in range(blocks):
-            msq[s, a:a + 1, :] = mass_ref[s:s + 1, a * 128:(a + 1) * 128]
+            msq[s, a:a + 1, :] = mass[s:s + 1, a * 128:(a + 1) * 128]
     lax.fori_loop(0, count, weigh, 0)
     send_owners(1)
 
@@ -210,11 +226,11 @@
             got = [rmap_s[r, j // count, 0, 3 * (j % count) + i] for i in range(3)]
             mine = got[0] // BPO == me
             found = [jnp.where(mine, g - me * BPO, f) for g, f in zip(got, found)]
-        for i in range(3):
-            table_ref[r, i] = found[i]
+        table[pl.ds(r, 1)] = as_row(found)
         return carry
 
     lax.fori_loop(0, owners, place, 0)
+    table_copy = pltpu.make_async_copy(table, table_hbm, table_sem)
 
     loads["fix"].wait()
 
@@ -225,10 +241,12 @@
     lax.fori_loop(0, count, couple, 0)
     coup_copy = pltpu.make_async_copy(coup, coup_hbm, coup_sem)
     coup_copy.start()
+    table_copy.start()
     send_owners(4)
     send_owners(5)
 
     coup_copy.wait()
+    table_copy.wait()
     for d in range(1, lanes):
         map_sends[d - 1].wait_send()
     pltpu.make_async_copy(rmap.at[pl.ds(0, owners - 1)], rmap.at[pl.ds(0, owners - 1)], rm_send).wait()
@@ -241,39 +259,66 @@
         pltpu.make_async_copy(sent, sent, x_recv.at[c]).wait()
 
 
-def assemble(owners, table_ref, recv_hbm, k_ref, m_ref, buf, sem):
-    def fetch(r):
-        return pltpu.make_async_copy(recv_hbm.at[r], buf.at[r], sem.at[r])
-
-    def begin(r, carry):
-        @pl.when(table_ref[r, 0] >= 0)
-        def _():
-            fetch(r).start()
-
-        return carry
-
-    lax.fori_loop(0, owners, begin, 0)
+def assemble(
+    owners, table_hbm, recv_hbm, coup_hbm, k_hbm, m_hbm, coup_out,
+    table, buf, k_acc, m_acc, coup, table_sem, k_sem, m_sem, out_sem, coup_in, coup_back,
+):
+    half = len(PAIRS)
+    to_scalars = pltpu.make_async_copy(table_hbm, table, table_sem)
+    to_scalars.start()
+
+    def fetch(r, mat, sem):
+        planes = pl.ds(mat * half, half)
+        return pltpu.make_async_copy(recv_hbm.at[r, planes], buf.at[r, planes], sem.at[r])
+
+    def begin(mat, sem):
+        def one(r, carry):
+            fetch(r, mat, sem).start()
+            return carry
+
+        lax.fori_loop(0, owners, one, 0)
+
+    begin(0, k_sem)
+    begin(1, m_sem)
+    take = pltpu.make_async_copy(coup_hbm, coup, coup_in)
+    take.start()
 
     def clear(e, carry):
-        k_ref[e] = jnp.zeros(k_ref.shape[1:], jnp.float32)
-        m_ref[e] = jnp.zeros(m_ref.shape[1:], jnp.float32)
+        k_acc[e] = jnp.zeros(k_acc.shape[1:], jnp.float32)
+        m_acc[e] = jnp.zeros(m_acc.shape[1:], jnp.float32)
         return carry
 
     lax.fori_loop(0, BPO * BAND, clear, 0)
-
-    def add(r, carry):
-        @pl.when(table_ref[r, 0] >= 0)
-        def _():
-            places = [table_ref[r, i] for i in range(3)]
-            fetch(r).wait()
-            for p, (i, j) in enumerate(PAIRS):
-                e = places[i] * BAND + places[j] - places[i]
-                k_ref[e] += buf[r, p]
-                m_ref[e] += buf[r, len(PAIRS) + p]
-
-        return carry
-
-    lax.fori_loop(0, owners, add, 0)
+    to_scalars.wait()
+
+    def add(acc, mat, sem):
+        def one(r, carry):
+            fetch(r, mat, sem).wait()
+            places = [table[r, 0, i] for i in range(3)]
+
+            @pl.when(places[0] >= 0)
+            def _():
+                entries = [places[i] * BAND + places[j] - places[i] for i, j in PAIRS]
+                sums = [acc[e] + buf[r, mat * half + p] for p, e in enumerate(entries)]
+                for e, total in zip(entries, sums):
+                    acc[e] = total
+
+            return carry
+
+        lax.fori_loop(0, owners, one, 0)
+
+    add(k_acc, 0, k_sem)
+    k_out = pltpu.make_async_copy(k_acc, k_hbm, out_sem.at[0])
+    k_out.start()
+    take.wait()
+    give = pltpu.make_async_copy(coup, coup_out, coup_back)
+    give.start()
+    add(m_acc, 1, m_sem)
+    m_out = pltpu.make_async_copy(m_acc, m_hbm, out_sem.at[1])
+    m_out.start()
+    k_out.wait()
+    give.wait()
+    m_out.wait()
 
 
 def per_device(stiff_bb, stiff_bi, constraint_modes, interior_mass, fixed_modes, mass_bb, boundary_map):
@@ -283,21 +328,19 @@
     width = order // 3
     part = width // lanes
     planes = 2 * len(PAIRS)
-    maps = jnp.pad(boundary_map.reshape(1, 1, 3 * count), ((0, 0), (0, 0), (0, 128 - 3 * count)))
 
     anywhere = pl.BlockSpec(memory_space=pl.ANY)
-    in_vmem = pl.BlockSpec(memory_space=pltpu.VMEM)
     f32, bf16, i32 = jnp.float32, jnp.bfloat16, jnp.int32
     dma = pltpu.SemaphoreType.DMA
     received, table, coupling = pl.pallas_call(
         functools.partial(reduce_and_send, owners, lanes),
         out_shape=(
             jax.ShapeDtypeStruct((owners, planes, part, width), f32),
-            jax.ShapeDtypeStruct((owners, 4), i32),
+            jax.ShapeDtypeStruct((owners, 1, 128), i32),
             jax.ShapeDtypeStruct((count, modes, order), f32),
         ),
-        in_specs=[in_vmem, in_vmem] + [anywhere] * 5,
-        out_specs=(anywhere, pl.BlockSpec(memory_space=pltpu.SMEM), anywhere),
+        in_specs=[anywhere] * 7,
+        out_specs=(anywhere, anywhere, anywhere),
         scratch_shapes=[
             pltpu.VMEM((count, inner, order), bf16),
             pltpu.VMEM((count, order, inner), bf16),
@@ -305,37 +348,53 @@
             pltpu.VMEM((count, inner, order), bf16),
             pltpu.VMEM((count, 3, width, order), bf16),
             pltpu.VMEM((count, 3, width, order), bf16),
+            pltpu.VMEM((count, inner), f32),
             pltpu.VMEM((count, 128, 128), f32),
             pltpu.VMEM((count, modes, order), f32),
+            pltpu.SMEM((count, 3), i32),
+            pltpu.VMEM((1, 1, 128), i32),
             pltpu.VMEM((lanes, 1, 128), i32),
             pltpu.SMEM((lanes, 1, 128), i32),
             pltpu.VMEM((owners, lanes, 1, 128), i32),
             pltpu.SMEM((owners, lanes, 1, 128), i32),
             pltpu.SMEM((owners,), i32),
+            pltpu.VMEM((owners, 1, 128), i32),
         ]
         + [pltpu.VMEM((count, n, width, width), f32) for _, _, _, n in CHUNKS]
         + [pltpu.VMEM((count * lanes, n, part, width), f32) for _, _, _, n in CHUNKS]
         + [pltpu.VMEM((owners, n, part, width), f32) for _, _, _, n in CHUNKS]
         + [
-            dma((9,)), dma, dma((lanes - 1,)), dma((lanes - 1,)), dma, dma, dma, dma,
+            dma((13,)), dma, dma, dma((lanes - 1,)), dma((lanes - 1,)), dma, dma, dma, dma,
             dma((len(CHUNKS), lanes - 1)), dma((len(CHUNKS), lanes - 1)),
             dma((len(CHUNKS),)), dma((len(CHUNKS),)), dma((len(CHUNKS),)),
         ],
         compiler_params=pltpu.CompilerParams(
             collective_id=0, has_side_effects=True, vmem_limit_bytes=60 * 1024 * 1024),
         name="reduce_and_send",
-    )(maps, interior_mass, stiff_bb, stiff_bi, constraint_modes, fixed_modes, mass_bb)
-
-    entry = jax.ShapeDtypeStruct((BPO * BAND, part, width), f32)
-    k_band, m_band = pl.pallas_call(
+    )(boundary_map, interior_mass, stiff_bb, stiff_bi, constraint_modes, fixed_modes, mass_bb)
+
+    entry = (BPO * BAND, part, width)
+    in_hbm = pl.BlockSpec(memory_space=pltpu.HBM)
+    k_band, m_band, coupling = pl.pallas_call(
         functools.partial(assemble, owners),
-        out_shape=(entry, entry),
-        in_specs=[pl.BlockSpec(memory_space=pltpu.SMEM), anywhere],
-        out_specs=(in_vmem, in_vmem),
-        scratch_shapes=[pltpu.VMEM((owners, planes, part, width), f32), dma((owners,))],
-        compiler_params=pltpu.CompilerParams(vmem_limit_bytes=40 * 1024 * 1024),
+        out_shape=(
+            jax.ShapeDtypeStruct(entry, f32),
+            jax.ShapeDtypeStruct(entry, f32),
+            jax.ShapeDtypeStruct((count, modes, order), f32),
+        ),
+        in_specs=[in_hbm] * 3,
+        out_specs=[in_hbm] * 3,
+        scratch_shapes=[
+            pltpu.SMEM((owners, 1, 128), i32),
+            pltpu.VMEM((owners, planes, part, width), f32),
+            pltpu.VMEM(entry, f32),
+            pltpu.VMEM(entry, f32),
+            pltpu.VMEM((count, modes, order), f32),
+            dma, dma((owners,)), dma((owners,)), dma((2,)), dma, dma,
+        ],
+        compiler_params=pltpu.CompilerParams(vmem_limit_bytes=60 * 1024 * 1024),
         name="assemble",
-    )(table, received)
+    )(table, received, coupling)
     banded = (BPO, BAND, part, width)
     return k_band.reshape(banded), m_band.reshape(banded), coupling
 

time: 106 us -> 94.6 us (0.89)
  Pallas kernels: 100 us -> 93.8 us
  local copies, waits for them, and re-layouts: 5.8 us -> 0 us
    pallas_call x1, Pallas kernels: 10.7 us -> 6.1 us  [per_device(): pl.pallas_call(functools.partial(assemble, owners), out_shape=(jax.ShapeD...]
    unnamed x7 -> x0, local copies, waits for them, and re-layouts: 4.51 us -> none
    pallas_call x1, Pallas kernels: 89.5 us -> 87.7 us  [per_device(): pl.pallas_call(functools.partial(reduce_and_send, owners, lanes), out_sha...]
where the time goes in v2:
time: 94.6 us; the launch traced here: 94.5 us
  Pallas kernels  93.8 us (99%)
    pallas_call x1, Pallas kernels, per_device(): pl.pallas_call(functools.partial(reduce_and_send, owners, lanes), out_sha...  87.7 us
    pallas_call x1, Pallas kernels, per_device(): pl.pallas_call(functools.partial(assemble, owners), out_shape=(jax.ShapeD...  6.1 us

profile of v2, /device:TPU:1, one launch (start us, length us, event | category | flops | bytes accessed | tf_op | source)
XLA Modules:
  0.0 94.5 jit_solution(11495363659580037254)
XLA Ops:
  0.6 87.7 %reduce_and_send.1 = (f32[32,12,32,128]{3,2,1,0:T(8,128)}, s32[32,1,128]{2,1,0:T(1,128)}, f32[3,256,384]{2,1,0:T(8,128)}) custom-call(s32[3,3]{1,0:T(4,128)} %map_hbm.1, f32[3,3072]{1,0:T(4,128)} %mass_hbm.1, bf16[3,3,128,384]{3,2,1,0:T(8,128)(2,1)} %sbb_hbm.1, bf16[3,384,3072]{2,1,0:T(8,128)(2,1)} %sbi_hbm.1, bf16[3,3072,384]{2,1,0:T(8,128)(2,1)} %psi_hbm.1, ...), custom_call_target="tpu_custom_call" | custom-call | tf_op jit(solution)/shard_map/reduce_and_send/pallas_call | solution.py:335
  88.3 6.1 %assemble.1 = (f32[96,32,128]{2,1,0:T(8,128)}, f32[96,32,128]{2,1,0:T(8,128)}, f32[3,256,384]{2,1,0:T(8,128)}) custom-call(s32[32,1,128]{2,1,0:T(1,128)} %get-tuple-element.9.table_hbm, f32[32,12,32,128]{3,2,1,0:T(8,128)} %get-tuple-element.10.recv_hbm, f32[3,256,384]{2,1,0:T(8,128)} %get-tuple-element.11.coup_hbm), custom_call_target="tpu_custom_call" | custom-call | tf_op jit(solution)/shard_map/assemble/pallas_call | solution.py:378

commit v3 on v2

v3 whole, which is shorter than its diff:
```python
import functools

import jax
import jax.numpy as jnp
from jax import lax
from jax.experimental import pallas as pl
from jax.experimental.pallas import tpu as pltpu
from jax.sharding import PartitionSpec as P

BAND = 4
LAGS = (1, 3)
BPO = 24
MESH = pl.DeviceIdType.MESH

PAIRS = ((2, 2), (1, 1), (1, 2), (0, 0), (0, 1), (0, 2))
BLOCKS = ((0, 2), (0, 1), (0, 0), (1, 0), (1, 1), (1, 2))
CHUNKS = tuple(
    (i, q, mat * len(PAIRS) + (0, 1, 3)[2 - b] + q) for i, (mat, b) in enumerate(BLOCKS) for q in range(3 - b)
)


def row_of(y, x, k):
    return y * 8 + x * 2 + k


def place(h, f, g, k):
    return row_of(f, g, k) if h == 0 else row_of(g, f, k)


def owner_of(block):
    return lax.shift_right_logical(block * 2731, jnp.int32(16))


def first_axis(h, owner):
    return lax.shift_right_logical(owner, jnp.int32(3)) if h == 0 else lax.shift_right_logical(owner, jnp.int32(1)) & 3


def count_before(flags):
    total, before = jnp.int32(0), []
    for flag in flags:
        before.append(total)
        total = total + jnp.where(flag, 1, 0)
    return before, total


def find(keys, values, wanted):
    found = jnp.int32(0)
    for key, value in zip(keys, values):
        found = jnp.where(key == wanted, value, found)
    return found


def reduce_and_send(
    owners, lanes,
    map_hbm, mass_hbm, sbb_hbm, sbi_hbm, psi_hbm, fix_hbm, mbb_hbm,
    recv0_hbm, recv1_hbm, table_hbm, coup_hbm,
    psi, sbi, fix, wgt, sbb, mbb, mass, msq, coup, map_s, mine, zmap, whole, whole_s, rmap, rmap_s, pick1, pick2, table,
    *rest,
):
    n_chunks = len(CHUNKS)
    reds, rest = rest[:len(BLOCKS)], rest[len(BLOCKS):]
    zs, firsts, arrived, seconds = (rest[i * n_chunks:(i + 1) * n_chunks] for i in range(4))
    (in_sem, coup_sem, table_sem, zm_send, zm_recv, zm_loc, rm_send, rm_recv, rm_loc,
     z_send, z_recv, f_send, f_recv, p_send, p_recv, x_send, x_recv, x_own) = rest[4 * n_chunks:]
    recvs = (recv0_hbm, recv1_hbm)
    me, lane = lax.axis_index("row"), lax.axis_index("col")
    y, x, core = me // 8, (me // 2) % 4, me % 2
    at = [(y, x), (x, y)]
    beside = [[place(h, (f + step) % 4, g, core) for step in (1, 3)] for h, (f, g) in enumerate(at)]
    line = [[place(h, f, (g + t // 2) % 4, (core + t) % 2) for t in range(8)] for h, (f, g) in enumerate(at)]
    from_here = [pl.ds((g * 2 + core) * 4, 4) for _, g in at]
    count, order = psi.shape[0], psi.shape[2]
    width = order // 3
    part = width // lanes
    half = part // 2
    group = lanes * count

    loads = {}

    def load(name, src, dst):
        loads[name] = pltpu.make_async_copy(src, dst, in_sem.at[len(loads)])
        loads[name].start()

    def load_block(b):
        cols = pl.ds(b * width, width)
        load(("psi", b), psi_hbm.at[:, :, cols], psi.at[:, :, cols])
        load(("sbi", b), sbi_hbm.at[:, cols, :], sbi.at[:, cols, :])
        load(("sbb", b), sbb_hbm.at[:, b], sbb.at[:, b])

    def loaded(b):
        for name in ("psi", "sbi", "sbb"):
            loads[name, b].wait()

    load("map", map_hbm, map_s)
    load_block(2)

    barrier = pltpu.get_barrier_semaphore()
    for d in range(1, lanes):
        pl.semaphore_signal(barrier, inc=1, device_id=(me, lax.rem(lane + d, lanes)), device_id_type=MESH)

    def greet(t, carry):
        pl.semaphore_signal(barrier, inc=1, device_id=(lax.rem(me + t, owners), lane), device_id_type=MESH)
        return carry

    lax.fori_loop(1, owners, greet, 0)

    loads["map"].wait()
    lanes_of = lax.broadcasted_iota(jnp.int32, (1, 1, 128), 2)

    def as_row(scalars, offset):
        row = jnp.zeros((1, 1, 128), jnp.int32)
        for i, scalar in enumerate(scalars):
            row = jnp.where(lanes_of == offset + i, scalar, row)
        return row

    own = as_row([map_s[s, i] for s in range(count) for i in range(3)], 3 * count * lane)
    mine[...] = own
    zmap[pl.ds(lane, 1)] = own
    pl.semaphore_wait(barrier, owners + lanes - 2)
    map_sends = []
    for d in range(1, lanes):
        peer = lax.rem(lane + d, lanes)
        copy = pltpu.make_async_remote_copy(
            src_ref=mine, dst_ref=zmap.at[pl.ds(lane, 1)], send_sem=zm_send.at[d - 1],
            recv_sem=zm_recv.at[d - 1], device_id=(me, peer), device_id_type=MESH)
        copy.start()
        map_sends.append(copy)

    def stiff_block(b, red):
        n = 3 - b

        def one(s, carry):
            out = jnp.dot(sbi[s, pl.ds(b * width, width), :], psi[s, :, pl.ds(b * width, n * width)],
                          preferred_element_type=jnp.float32)
            out = out + sbb[s, b, :, pl.ds(b * width, n * width)].astype(jnp.float32)
            for q in range(n):
                red[s, q] = out[:, q * width:(q + 1) * width]
            return carry

        lax.fori_loop(0, count, one, 0)

    def mass_block(b, red):
        n = 3 - b

        def one(s, carry):
            out = lax.dot_general(psi[s, :, pl.ds(b * width, width)], wgt[s, :, pl.ds(b * width, n * width)],
                                  (((0,), (0,)), ((), ())), preferred_element_type=jnp.float32)
            out = out + mbb[s, b, :, pl.ds(b * width, n * width)].astype(jnp.float32)
            for q in range(n):
                red[s, q] = out[:, q * width:(q + 1) * width]
            return carry

        lax.fori_loop(0, count, one, 0)

    z_copies, f_copies, p_copies = {}, {}, {}

    def send_lanes(c):
        red, q, z = reds[CHUNKS[c][0]], CHUNKS[c][1], zs[c]
        ours = pl.ds(count * lane, count)
        for h in range(2):
            z[ours, h] = red[:, q, pl.ds(pl.multiple_of(part * lane + half * h, half), half), :]
        for d in range(1, lanes):
            peer = lax.rem(lane + d, lanes)
            for h in range(2):
                copy = pltpu.make_async_remote_copy(
                    src_ref=red.at[:, q, pl.ds(pl.multiple_of(part * peer + half * h, half), half), :],
                    dst_ref=z.at[ours, h], send_sem=z_send.at[c, h, d - 1],
                    recv_sem=z_recv.at[c, h, d - 1], device_id=(me, peer), device_id_type=MESH)
                copy.start()
                z_copies[c, h, d] = copy

    def first_leg(c):
        z, first = zs[c], firsts[c]
        for copy in [z_copies[c, h, d] for h in range(2) for d in range(1, lanes)]:
            copy.wait_recv()
        for h in range(2):
            slots = [z[pick1[h * 16 + t], h] for t in range(16)]
            for t in range(16):
                first[h, t] = slots[t]
        for h in range(2):
            for way in range(2):
                copy = pltpu.make_async_remote_copy(
                    src_ref=first.at[h, pl.ds(8 * way, 8)], dst_ref=arrived[c].at[h, pl.ds(8 * way, 8)],
                    send_sem=f_send.at[c, h, way], recv_sem=f_recv.at[c, h, way],
                    device_id=(beside[h][way], lane), device_id_type=MESH)
                copy.start()
                f_copies[c, h, way] = copy

    def pass_on(c):
        for h in range(2):
            for way in range(2):
                f_copies[c, h, way].wait_recv()
                copy = pltpu.make_async_remote_copy(
                    src_ref=arrived[c].at[h, pl.ds(8 * way + 4, 4)], dst_ref=arrived[c].at[h, pl.ds(16 + 4 * way, 4)],
                    send_sem=p_send.at[c, h, way], recv_sem=p_recv.at[c, h, way],
                    device_id=(beside[h][way], lane), device_id_type=MESH)
                copy.start()
                p_copies[c, h, way] = copy

    def own_copy(c, h):
        return pltpu.make_async_copy(
            seconds[c].at[h, pl.ds(0, 4)], recvs[h].at[from_here[h], CHUNKS[c][2]], x_own.at[c, h])

    def second_leg(c):
        z, second = zs[c], seconds[c]
        for copy in [p_copies[c, h, way] for h in range(2) for way in range(2)]:
            copy.wait_recv()
        for h in range(2):
            for low in (0, 16):
                picked = [
                    z[pick2[h * 32 + i], h] if i % 4 == 0 else arrived[c][h, pick2[h * 32 + i]]
                    for i in range(low, low + 16)
                ]
                for i, value in enumerate(picked):
                    second[h, low + i] = value
            own_copy(c, h).start()
        for t in range(1, 8):
            for h in range(2):
                pltpu.make_async_remote_copy(
                    src_ref=second.at[h, pl.ds(t * 4, 4)], dst_ref=recvs[h].at[from_here[h], CHUNKS[c][2]],
                    send_sem=x_send.at[c, h], recv_sem=x_recv.at[c, h],
                    device_id=(line[h][t], lane), device_id_type=MESH).start()

    def first_tables():
        heads = [owner_of(whole_s[0, 0, 3 * j]) for j in range(group)]
        numbers = [jnp.int32(j) for j in range(group)]
        for h in range(2):
            f = at[h][0]
            away = [(first_axis(h, head) + 4 - f) & 3 for head in heads]
            near, n1 = count_before([a == 1 for a in away])
            far, n2 = count_before([a == 2 for a in away])
            back, _ = count_before([a == 3 for a in away])
            split = jnp.minimum(jnp.minimum(n2, 8 - n1), 4)
            plus = [jnp.where(a == 1, r1, jnp.where((a == 2) & (r2 < split), 7 - r2, -1))
                    for a, r1, r2 in zip(away, near, far)]
            minus = [jnp.where(a == 3, r3, jnp.where((a == 2) & (r2 >= split), 7 + split - r2, -1))
                     for a, r3, r2 in zip(away, back, far)]
            for t in range(8):
                pick1[h * 16 + t] = find(plus, numbers, t)
                pick1[h * 16 + 8 + t] = find(minus, numbers, t)
            for t in range(8):
                pick2[h * 32 + t * 4] = find(heads, numbers, line[h][t])

    def second_tables():
        for h in range(2):
            f, g = at[h]
            for d in range(1, 4):
                source = place(h, (f + 4 - d) % 4, g, core)
                heads = [owner_of(rmap_s[source, 0, 3 * j]) for j in range(group)]
                axis = [first_axis(h, head) for head in heads]
                rank, n2 = count_before([a == f for a in axis])
                if d == 1:
                    spot = rank
                elif d == 3:
                    spot = [8 + r for r in rank]
                else:
                    _, n1 = count_before([a == (f + 3) % 4 for a in axis])
                    split = jnp.minimum(jnp.minimum(n2, 8 - n1), 4)
                    spot = [jnp.where(r < split, 19 - r, 23 + split - r) for r in rank]
                for t in range(8):
                    pick2[h * 32 + t * 4 + d] = find(heads, spot, line[h][t])

    def step(c):
        if c < n_chunks:
            first_leg(c)
        if 0 <= c - LAGS[0] < n_chunks:
            pass_on(c - LAGS[0])
        if 0 <= c - LAGS[1] < n_chunks:
            second_leg(c - LAGS[1])

    loaded(2)
    load_block(1)
    stiff_block(2, reds[0])
    send_lanes(0)
    loaded(1)
    load_block(0)
    stiff_block(1, reds[1])
    send_lanes(1)
    send_lanes(2)

    for d in range(1, lanes):
        map_sends[d - 1].wait_recv()
    merged = zmap[0:1]
    for i in range(1, lanes):
        merged = merged + zmap[i:i + 1]
    whole[...] = merged
    rmap[pl.ds(me, 1)] = merged
    to_scalars = pltpu.make_async_copy(whole, whole_s, zm_loc)
    to_scalars.start()

    to_scalars.wait()
    first_tables()
    step(0)

    def tell(t, carry):
        pltpu.make_async_remote_copy(
            src_ref=whole, dst_ref=rmap.at[pl.ds(me, 1)], send_sem=rm_send, recv_sem=rm_recv,
            device_id=(lax.rem(me + t, owners), lane), device_id_type=MESH).start()
        return carry

    lax.fori_loop(1, owners, tell, 0)
    loaded(0)
    load("mass", mass_hbm, mass)
    load("mbb", mbb_hbm, mbb)
    load("fix", fix_hbm, fix)
    stiff_block(0, reds[2])
    for c in (3, 4, 5):
        send_lanes(c)
    step(1)

    others = rmap.at[pl.ds(0, owners - 1)]
    pltpu.make_async_copy(others, others, rm_recv).wait()
    to_scalars = pltpu.make_async_copy(rmap, rmap_s, rm_loc)
    to_scalars.start()
    to_scalars.wait()
    second_tables()
    step(2)

    blocks = psi.shape[1] // 128

    def weigh(s, carry):
        turned = msq[s].T
        for a in range(blocks):
            rows = slice(a * 128, (a + 1) * 128)
            wgt[s, rows, :] = (turned[:, a:a + 1] * psi[s, rows, :].astype(jnp.float32)).astype(jnp.bfloat16)
        return carry

    msq[...] = jnp.zeros_like(msq)
    loads["mass"].wait()
    for s in range(count):
        for a in range(blocks):
            msq[s, a:a + 1, :] = mass[s:s + 1, a * 128:(a + 1) * 128]
    lax.fori_loop(0, count, weigh, 0)

    step(3)
    loads["mbb"].wait()
    mass_block(0, reds[3])
    for c in (6, 7, 8):
        send_lanes(c)
    step(4)
    mass_block(1, reds[4])
    for c in (9, 10):
        send_lanes(c)
    step(5)
    mass_block(2, reds[5])
    send_lanes(11)
    step(6)

    def settle(r, carry):
        starts = [rmap_s[r, 0, 3 * j] - me * BPO for j in range(group)]
        which = jnp.int32(-1)
        for j, start in enumerate(starts):
            which = jnp.where((start >= 0) & (start < BPO), j, which)
        spot = 3 * jnp.maximum(which, 0)
        found = [jnp.where(which >= 0, rmap_s[r, 0, spot + i] - me * BPO, -1) for i in range(3)]
        table[pl.ds(r, 1)] = as_row(found, 0)
        return carry

    lax.fori_loop(0, owners, settle, 0)
    loads["fix"].wait()

    def couple(s, carry):
        coup[s] = lax.dot_general(fix[s], wgt[s], (((0,), (0,)), ((), ())), preferred_element_type=jnp.float32)
        return carry

    step(7)
    lax.fori_loop(0, 1, couple, 0)
    step(8)
    lax.fori_loop(1, 2, couple, 0)
    step(9)
    lax.fori_loop(2, count, couple, 0)
    coup_copy = pltpu.make_async_copy(coup, coup_hbm, coup_sem)
    coup_copy.start()
    table_copy = pltpu.make_async_copy(table, table_hbm, table_sem)
    table_copy.start()
    for c in range(10, n_chunks + LAGS[1]):
        step(c)

    coup_copy.wait()
    table_copy.wait()
    for d in range(1, lanes):
        map_sends[d - 1].wait_send()
    pltpu.make_async_copy(others, others, rm_send).wait()
    for copies in (z_copies, f_copies, p_copies):
        for copy in copies.values():
            copy.wait_send()
    for c in range(n_chunks):
        for h in range(2):
            own_copy(c, h).wait()
            sent = seconds[c].at[h, pl.ds(4, 28)]
            pltpu.make_async_copy(sent, sent, x_send.at[c, h]).wait()
            pltpu.make_async_copy(sent, sent, x_recv.at[c, h]).wait()


def assemble(
    owners, table_hbm, recv0_hbm, recv1_hbm, coup_hbm, k_hbm, m_hbm, coup_out,
    table, buf0, buf1, k_acc, m_acc, coup, table_sem, in_sem, out_sem, coup_in, coup_back,
):
    me = lax.axis_index("row")
    pairs = len(PAIRS)
    half = buf0.shape[2]
    to_scalars = pltpu.make_async_copy(table_hbm, table, table_sem)
    to_scalars.start()

    def begin(mat):
        def one(q, carry):
            slots, planes = pl.ds(q * 4, 4), pl.ds(mat * pairs, pairs)
            for src, dst, h in ((recv0_hbm, buf0, 0), (recv1_hbm, buf1, 1)):
                pltpu.make_async_copy(src.at[slots, planes], dst.at[slots, planes], in_sem.at[mat, h]).start()
            return carry

        lax.fori_loop(0, owners // 4, one, 0)

    def ready(mat):
        planes = pl.ds(mat * pairs, pairs)
        for src, dst, h in ((recv0_hbm, buf0, 0), (recv1_hbm, buf1, 1)):
            pltpu.make_async_copy(src.at[:, planes], dst.at[:, planes], in_sem.at[mat, h]).wait()

    begin(0)
    begin(1)
    take = pltpu.make_async_copy(coup_hbm, coup, coup_in)
    take.start()

    def clear(e, carry):
        k_acc[e] = jnp.zeros(k_acc.shape[1:], jnp.float32)
        m_acc[e] = jnp.zeros(m_acc.shape[1:], jnp.float32)
        return carry

    lax.fori_loop(0, BPO * BAND, clear, 0)
    to_scalars.wait()

    def add(acc, mat):
        def one(r, carry):
            places = [table[r, 0, i] for i in range(3)]
            y, x, k = r // 8, (r // 2) % 4, r % 2
            spots = ((x * 2 + k) * 4 + (me // 8 + 4 - y) % 4, (y * 2 + k) * 4 + ((me // 2) % 4 + 4 - x) % 4)

            @pl.when(places[0] >= 0)
            def _():
                entries = [places[i] * BAND + places[j] - places[i] for i, j in PAIRS]
                sums = [
                    acc[e, h * half:(h + 1) * half, :] + buf[spots[h], mat * pairs + p]
                    for p, e in enumerate(entries) for h, buf in enumerate((buf0, buf1))
                ]
                for i, total in enumerate(sums):
                    h = i % 2
                    acc[entries[i // 2], h * half:(h + 1) * half, :] = total

            return carry

        lax.fori_loop(0, owners, one, 0)

    ready(0)
    add(k_acc, 0)
    k_out = pltpu.make_async_copy(k_acc, k_hbm, out_sem.at[0])
    k_out.start()
    take.wait()
    give = pltpu.make_async_copy(coup, coup_out, coup_back)
    give.start()
    ready(1)
    add(m_acc, 1)
    m_out = pltpu.make_async_copy(m_acc, m_hbm, out_sem.at[1])
    m_out.start()
    k_out.wait()
    give.wait()
    m_out.wait()


def per_device(stiff_bb, stiff_bi, constraint_modes, interior_mass, fixed_modes, mass_bb, boundary_map):
    owners, lanes = lax.axis_size("row"), lax.axis_size("col")
    count, inner, order = constraint_modes.shape
    modes = fixed_modes.shape[2]
    width = order // 3
    part = width // lanes
    half = part // 2
    group = lanes * count
    planes = 2 * len(PAIRS)

    anywhere = pl.BlockSpec(memory_space=pl.ANY)
    f32, bf16, i32 = jnp.float32, jnp.bfloat16, jnp.int32
    dma = pltpu.SemaphoreType.DMA
    received0, received1, table, coupling = pl.pallas_call(
        functools.partial(reduce_and_send, owners, lanes),
        out_shape=(
            jax.ShapeDtypeStruct((owners, planes, half, width), f32),
            jax.ShapeDtypeStruct((owners, planes, half, width), f32),
            jax.ShapeDtypeStruct((owners, 1, 128), i32),
            jax.ShapeDtypeStruct((count, modes, order), f32),
        ),
        in_specs=[anywhere] * 7,
        out_specs=(anywhere,) * 4,
        scratch_shapes=[
            pltpu.VMEM((count, inner, order), bf16),
            pltpu.VMEM((count, order, inner), bf16),
            pltpu.VMEM((count, inner, modes), bf16),
            pltpu.VMEM((count, inner, order), bf16),
            pltpu.VMEM((count, 3, width, order), bf16),
            pltpu.VMEM((count, 3, width, order), bf16),
            pltpu.VMEM((count, inner), f32),
            pltpu.VMEM((count, 128, 128), f32),
            pltpu.VMEM((count, modes, order), f32),
            pltpu.SMEM((count, 3), i32),
            pltpu.VMEM((1, 1, 128), i32),
            pltpu.VMEM((lanes, 1, 128), i32),
            pltpu.VMEM((1, 1, 128), i32),
            pltpu.SMEM((1, 1, 128), i32),
            pltpu.VMEM((owners, 1, 128), i32),
            pltpu.SMEM((owners, 1, 128), i32),
            pltpu.SMEM((32,), i32),
            pltpu.SMEM((64,), i32),
            pltpu.VMEM((owners, 1, 128), i32),
        ]
        + [pltpu.VMEM((count, 3 - b, width, width), f32) for _, b in BLOCKS]
        + [pltpu.VMEM((group, 2, half, width), f32)] * len(CHUNKS)
        + [pltpu.VMEM((2, 16, half, width), f32)] * len(CHUNKS)
        + [pltpu.VMEM((2, 24, half, width), f32)] * len(CHUNKS)
        + [pltpu.VMEM((2, 32, half, width), f32)] * len(CHUNKS)
        + [
            dma((13,)), dma, dma, dma((lanes - 1,)), dma((lanes - 1,)), dma, dma, dma, dma,
            dma((len(CHUNKS), 2, lanes - 1)), dma((len(CHUNKS), 2, lanes - 1)),
            dma((len(CHUNKS), 2, 2)), dma((len(CHUNKS), 2, 2)), dma((len(CHUNKS), 2, 2)), dma((len(CHUNKS), 2, 2)),
            dma((len(CHUNKS), 2)), dma((len(CHUNKS), 2)), dma((len(CHUNKS), 2)),
        ],
        compiler_params=pltpu.CompilerParams(
            collective_id=0, has_side_effects=True, vmem_limit_bytes=60 * 1024 * 1024),
        name="reduce_and_send",
    )(boundary_map, interior_mass, stiff_bb, stiff_bi, constraint_modes, fixed_modes, mass_bb)

    entry = (BPO * BAND, part, width)
    in_hbm = pl.BlockSpec(memory_space=pltpu.HBM)
    k_band, m_band, coupling = pl.pallas_call(
        functools.partial(assemble, owners),
        out_shape=(
            jax.ShapeDtypeStruct(entry, f32),
            jax.ShapeDtypeStruct(entry, f32),
            jax.ShapeDtypeStruct((count, modes, order), f32),
        ),
        in_specs=[in_hbm] * 4,
        out_specs=[in_hbm] * 3,
        scratch_shapes=[
            pltpu.SMEM((owners, 1, 128), i32),
            pltpu.VMEM((owners, planes, half, width), f32),
            pltpu.VMEM((owners, planes, half, width), f32),
            pltpu.VMEM(entry, f32),
            pltpu.VMEM(entry, f32),
            pltpu.VMEM((count, modes, order), f32),
            dma, dma((2, 2)), dma((2,)), dma, dma,
        ],
        compiler_params=pltpu.CompilerParams(vmem_limit_bytes=60 * 1024 * 1024),
        name="assemble",
    )(table, received0, received1, coupling)
    banded = (BPO, BAND, part, width)
    return k_band.reshape(banded), m_band.reshape(banded), coupling


def solution(mesh):
    both = ("row", "col")
    return jax.shard_map(
        per_device,
        mesh=mesh,
        in_specs=(
            P(both, None, None, None), P(both, None, None), P(both, None, None), P(both, None),
            P(both, None, None), P(both, None, None, None), P(both, None),
        ),
        out_specs=(P("row", None, "col", None), P("row", None, "col", None), P(both, None, None)),
        check_vma=False,
    )
```

time: 94.6 us -> 89.9 us (0.950)
  Pallas kernels: 93.8 us -> 89 us
    pallas_call x1, Pallas kernels: 87.7 us -> 83.8 us  [per_device(): pl.pallas_call(functools.partial(reduce_and_send, owners, lanes), out_sha...]
where the time goes in v3:
time: 89.9 us; the launch traced here: 89.8 us
  Pallas kernels  89 us (99%)
    pallas_call x1, Pallas kernels, per_device(): pl.pallas_call(functools.partial(reduce_and_send, owners, lanes), out_sha...  83.8 us
    pallas_call x1, Pallas kernels, per_device(): pl.pallas_call(functools.partial(assemble, owners), out_shape=(jax.ShapeD...  5.19 us

profile of v3, /device:TPU:1, one launch (start us, length us, event | category | flops | bytes accessed | tf_op | source)
XLA Modules:
  0.0 89.8 jit_solution(12218610658570544908)
XLA Ops:
  0.6 83.8 %reduce_and_send.1 = (f32[32,12,16,128]{3,2,1,0:T(8,128)}, f32[32,12,16,128]{3,2,1,0:T(8,128)}, s32[32,1,128]{2,1,0:T(1,128)}, f32[3,256,384]{2,1,0:T(8,128)}) custom-call(s32[3,3]{1,0:T(4,128)} %map_hbm.1, f32[3,3072]{1,0:T(4,128)} %mass_hbm.1, bf16[3,3,128,384]{3,2,1,0:T(8,128)(2,1)} %sbb_hbm.1, bf16[3,384,3072]{2,1,0:T(8,128)(2,1)} %sbi_hbm.1, ...), custom_call_target="tpu_custom_call" | custom-call | tf_op jit(solution)/shard_map/reduce_and_send/pallas_call | solution.py:482
  84.4 5.2 %assemble.1 = (f32[96,32,128]{2,1,0:T(8,128)}, f32[96,32,128]{2,1,0:T(8,128)}, f32[3,256,384]{2,1,0:T(8,128)}) custom-call(s32[32,1,128]{2,1,0:T(1,128)} %get-tuple-element.10.table_hbm, f32[32,12,16,128]{3,2,1,0:T(8,128)} %get-tuple-element.11.recv0_hbm, f32[32,12,16,128]{3,2,1,0:T(8,128)} %get-tuple-element.12.recv1_hbm, ...), custom_call_target="tpu_custom_call" | custom-call | tf_op jit(solution)/shard_map/assemble/pallas_call | solution.py:531

commit v4 on v3

--- a/solution.py
+++ b/solution.py
@@ -116,15 +116,6 @@
     own = as_row([map_s[s, i] for s in range(count) for i in range(3)], 3 * count * lane)
     mine[...] = own
     zmap[pl.ds(lane, 1)] = own
-    pl.semaphore_wait(barrier, owners + lanes - 2)
-    map_sends = []
-    for d in range(1, lanes):
-        peer = lax.rem(lane + d, lanes)
-        copy = pltpu.make_async_remote_copy(
-            src_ref=mine, dst_ref=zmap.at[pl.ds(lane, 1)], send_sem=zm_send.at[d - 1],
-            recv_sem=zm_recv.at[d - 1], device_id=(me, peer), device_id_type=MESH)
-        copy.start()
-        map_sends.append(copy)
 
     def stiff_block(b, red):
         n = 3 - b
@@ -271,6 +262,15 @@
     loaded(2)
     load_block(1)
     stiff_block(2, reds[0])
+    pl.semaphore_wait(barrier, owners + lanes - 2)
+    map_sends = []
+    for d in range(1, lanes):
+        peer = lax.rem(lane + d, lanes)
+        copy = pltpu.make_async_remote_copy(
+            src_ref=mine, dst_ref=zmap.at[pl.ds(lane, 1)], send_sem=zm_send.at[d - 1],
+            recv_sem=zm_recv.at[d - 1], device_id=(me, peer), device_id_type=MESH)
+        copy.start()
+        map_sends.append(copy)
     send_lanes(0)
     loaded(1)
     load_block(0)
@@ -352,7 +352,10 @@
         for j, start in enumerate(starts):
             which = jnp.where((start >= 0) & (start < BPO), j, which)
         spot = 3 * jnp.maximum(which, 0)
-        found = [jnp.where(which >= 0, rmap_s[r, 0, spot + i] - me * BPO, -1) for i in range(3)]
+        at_home = [rmap_s[r, 0, spot + i] - me * BPO for i in range(3)]
+        found = [
+            jnp.where(which >= 0, at_home[i] * BAND + at_home[j] - at_home[i], BPO * BAND) for i, j in PAIRS
+        ]
         table[pl.ds(r, 1)] = as_row(found, 0)
         return carry
 
@@ -426,40 +429,37 @@
         m_acc[e] = jnp.zeros(m_acc.shape[1:], jnp.float32)
         return carry
 
-    lax.fori_loop(0, BPO * BAND, clear, 0)
+    lax.fori_loop(0, BPO * BAND + 1, clear, 0)
     to_scalars.wait()
 
     def add(acc, mat):
-        def one(r, carry):
-            places = [table[r, 0, i] for i in range(3)]
-            y, x, k = r // 8, (r // 2) % 4, r % 2
-            spots = ((x * 2 + k) * 4 + (me // 8 + 4 - y) % 4, (y * 2 + k) * 4 + ((me // 2) % 4 + 4 - x) % 4)
-
-            @pl.when(places[0] >= 0)
-            def _():
-                entries = [places[i] * BAND + places[j] - places[i] for i, j in PAIRS]
-                sums = [
-                    acc[e, h * half:(h + 1) * half, :] + buf[spots[h], mat * pairs + p]
-                    for p, e in enumerate(entries) for h, buf in enumerate((buf0, buf1))
-                ]
-                for i, total in enumerate(sums):
-                    h = i % 2
-                    acc[entries[i // 2], h * half:(h + 1) * half, :] = total
-
+        def one(y, carry):
+            for g in range(4):
+                for k in range(2):
+                    r = y * 8 + g * 2 + k
+                    spots = ((g * 2 + k) * 4 + (me // 8 + 4 - y) % 4, (y * 2 + k) * 4 + (me // 2 + 4 - g) % 4)
+                    entries = [table[r, 0, p] for p in range(pairs)]
+                    sums = [
+                        acc[e, h * half:(h + 1) * half, :] + buf[spots[h], mat * pairs + p]
+                        for p, e in enumerate(entries) for h, buf in enumerate((buf0, buf1))
+                    ]
+                    for i, total in enumerate(sums):
+                        h = i % 2
+                        acc[entries[i // 2], h * half:(h + 1) * half, :] = total
             return carry
 
-        lax.fori_loop(0, owners, one, 0)
+        lax.fori_loop(0, 4, one, 0)
 
     ready(0)
     add(k_acc, 0)
-    k_out = pltpu.make_async_copy(k_acc, k_hbm, out_sem.at[0])
+    k_out = pltpu.make_async_copy(k_acc.at[pl.ds(0, BPO * BAND)], k_hbm, out_sem.at[0])
     k_out.start()
     take.wait()
     give = pltpu.make_async_copy(coup, coup_out, coup_back)
     give.start()
     ready(1)
     add(m_acc, 1)
-    m_out = pltpu.make_async_copy(m_acc, m_hbm, out_sem.at[1])
+    m_out = pltpu.make_async_copy(m_acc.at[pl.ds(0, BPO * BAND)], m_hbm, out_sem.at[1])
     m_out.start()
     k_out.wait()
     give.wait()
@@ -541,8 +541,8 @@
             pltpu.SMEM((owners, 1, 128), i32),
             pltpu.VMEM((owners, planes, half, width), f32),
             pltpu.VMEM((owners, planes, half, width), f32),
-            pltpu.VMEM(entry, f32),
-            pltpu.VMEM(entry, f32),
+            pltpu.VMEM((BPO * BAND + 1, part, width), f32),
+            pltpu.VMEM((BPO * BAND + 1, part, width), f32),
             pltpu.VMEM((count, modes, order), f32),
             dma, dma((2, 2)), dma((2,)), dma, dma,
         ],

time: 89.9 us -> 89.4 us (level)
  no operation moved by 1% of the time
where the time goes in v4:
time: 89.4 us; the launch traced here: 89.2 us
  Pallas kernels  88.4 us (99%)
    pallas_call x1, Pallas kernels, per_device(): pl.pallas_call(functools.partial(reduce_and_send, owners, lanes), out_sha...  83.4 us
    pallas_call x1, Pallas kernels, per_device(): pl.pallas_call(functools.partial(assemble, owners), out_shape=(jax.ShapeD...  5 us

profile of v4, /device:TPU:1, one launch (start us, length us, event | category | flops | bytes accessed | tf_op | source)
XLA Modules:
  0.0 89.2 jit_solution(15406944348851088091)
XLA Ops:
  0.6 83.4 %reduce_and_send.1 = (f32[32,12,16,128]{3,2,1,0:T(8,128)}, f32[32,12,16,128]{3,2,1,0:T(8,128)}, s32[32,1,128]{2,1,0:T(1,128)}, f32[3,256,384]{2,1,0:T(8,128)}) custom-call(s32[3,3]{1,0:T(4,128)} %map_hbm.1, f32[3,3072]{1,0:T(4,128)} %mass_hbm.1, bf16[3,3,128,384]{3,2,1,0:T(8,128)(2,1)} %sbb_hbm.1, bf16[3,384,3072]{2,1,0:T(8,128)(2,1)} %sbi_hbm.1, ...), custom_call_target="tpu_custom_call" | custom-call | tf_op jit(solution)/shard_map/reduce_and_send/pallas_call | solution.py:482
  84.0 5.0 %assemble.1 = (f32[96,32,128]{2,1,0:T(8,128)}, f32[96,32,128]{2,1,0:T(8,128)}, f32[3,256,384]{2,1,0:T(8,128)}) custom-call(s32[32,1,128]{2,1,0:T(1,128)} %get-tuple-element.10.table_hbm, f32[32,12,16,128]{3,2,1,0:T(8,128)} %get-tuple-element.11.recv0_hbm, f32[32,12,16,128]{3,2,1,0:T(8,128)} %get-tuple-element.12.recv1_hbm, ...), custom_call_target="tpu_custom_call" | custom-call | tf_op jit(solution)/shard_map/assemble/pallas_call | solution.py:531

commit v5 on v4

--- a/solution.py
+++ b/solution.py
@@ -190,7 +190,7 @@
 
     def own_copy(c, h):
         return pltpu.make_async_copy(
-            seconds[c].at[h, pl.ds(0, 4)], recvs[h].at[from_here[h], CHUNKS[c][2]], x_own.at[c, h])
+            seconds[c].at[h, pl.ds(0, 4)], recvs[h].at[CHUNKS[c][2], from_here[h]], x_own.at[c, h])
 
     def second_leg(c):
         z, second = zs[c], seconds[c]
@@ -205,10 +205,10 @@
                 for i, value in enumerate(picked):
                     second[h, low + i] = value
             own_copy(c, h).start()
-        for t in range(1, 8):
+        for t in (4, 5, 2, 6, 3, 7, 1):
             for h in range(2):
                 pltpu.make_async_remote_copy(
-                    src_ref=second.at[h, pl.ds(t * 4, 4)], dst_ref=recvs[h].at[from_here[h], CHUNKS[c][2]],
+                    src_ref=second.at[h, pl.ds(t * 4, 4)], dst_ref=recvs[h].at[CHUNKS[c][2], from_here[h]],
                     send_sem=x_send.at[c, h], recv_sem=x_recv.at[c, h],
                     device_id=(line[h][t], lane), device_id_type=MESH).start()
 
@@ -407,17 +407,17 @@
 
     def begin(mat):
         def one(q, carry):
-            slots, planes = pl.ds(q * 4, 4), pl.ds(mat * pairs, pairs)
+            plane = mat * pairs + q
             for src, dst, h in ((recv0_hbm, buf0, 0), (recv1_hbm, buf1, 1)):
-                pltpu.make_async_copy(src.at[slots, planes], dst.at[slots, planes], in_sem.at[mat, h]).start()
+                pltpu.make_async_copy(src.at[plane], dst.at[plane], in_sem.at[mat, h]).start()
             return carry
 
-        lax.fori_loop(0, owners // 4, one, 0)
+        lax.fori_loop(0, pairs, one, 0)
 
     def ready(mat):
         planes = pl.ds(mat * pairs, pairs)
         for src, dst, h in ((recv0_hbm, buf0, 0), (recv1_hbm, buf1, 1)):
-            pltpu.make_async_copy(src.at[:, planes], dst.at[:, planes], in_sem.at[mat, h]).wait()
+            pltpu.make_async_copy(src.at[planes], dst.at[planes], in_sem.at[mat, h]).wait()
 
     begin(0)
     begin(1)
@@ -440,7 +440,7 @@
                     spots = ((g * 2 + k) * 4 + (me // 8 + 4 - y) % 4, (y * 2 + k) * 4 + (me // 2 + 4 - g) % 4)
                     entries = [table[r, 0, p] for p in range(pairs)]
                     sums = [
-                        acc[e, h * half:(h + 1) * half, :] + buf[spots[h], mat * pairs + p]
+                        acc[e, h * half:(h + 1) * half, :] + buf[mat * pairs + p, spots[h]]
                         for p, e in enumerate(entries) for h, buf in enumerate((buf0, buf1))
                     ]
                     for i, total in enumerate(sums):
@@ -482,8 +482,8 @@
     received0, received1, table, coupling = pl.pallas_call(
         functools.partial(reduce_and_send, owners, lanes),
         out_shape=(
-            jax.ShapeDtypeStruct((owners, planes, half, width), f32),
-            jax.ShapeDtypeStruct((owners, planes, half, width), f32),
+            jax.ShapeDtypeStruct((planes, owners, half, width), f32),
+            jax.ShapeDtypeStruct((planes, owners, half, width), f32),
             jax.ShapeDtypeStruct((owners, 1, 128), i32),
             jax.ShapeDtypeStruct((count, modes, order), f32),
         ),
@@ -539,8 +539,8 @@
         out_specs=[in_hbm] * 3,
         scratch_shapes=[
             pltpu.SMEM((owners, 1, 128), i32),
-            pltpu.VMEM((owners, planes, half, width), f32),
-            pltpu.VMEM((owners, planes, half, width), f32),
+            pltpu.VMEM((planes, owners, half, width), f32),
+            pltpu.VMEM((planes, owners, half, width), f32),
             pltpu.VMEM((BPO * BAND + 1, part, width), f32),
             pltpu.VMEM((BPO * BAND + 1, part, width), f32),
             pltpu.VMEM((count, modes, order), f32),

time: 89.4 us -> 88.8 us (level)
  no operation moved by 1% of the time
where the time goes in v5:
time: 88.8 us; the launch traced here: 88.6 us
  Pallas kernels  87.9 us (99%)
    pallas_call x1, Pallas kernels, per_device(): pl.pallas_call(functools.partial(reduce_and_send, owners, lanes), out_sha...  83 us
    pallas_call x1, Pallas kernels, per_device(): pl.pallas_call(functools.partial(assemble, owners), out_shape=(jax.ShapeD...  4.88 us

profile of v5, /device:TPU:1, one launch (start us, length us, event | category | flops | bytes accessed | tf_op | source)
XLA Modules:
  0.0 88.6 jit_solution(15623772859884438699)
XLA Ops:
  0.6 83.0 %reduce_and_send.1 = (f32[12,32,16,128]{3,2,1,0:T(8,128)}, f32[12,32,16,128]{3,2,1,0:T(8,128)}, s32[32,1,128]{2,1,0:T(1,128)}, f32[3,256,384]{2,1,0:T(8,128)}) custom-call(s32[3,3]{1,0:T(4,128)} %map_hbm.1, f32[3,3072]{1,0:T(4,128)} %mass_hbm.1, bf16[3,3,128,384]{3,2,1,0:T(8,128)(2,1)} %sbb_hbm.1, bf16[3,384,3072]{2,1,0:T(8,128)(2,1)} %sbi_hbm.1, ...), custom_call_target="tpu_custom_call" | custom-call | tf_op jit(solution)/shard_map/reduce_and_send/pallas_call | solution.py:482
  83.7 4.9 %assemble.1 = (f32[96,32,128]{2,1,0:T(8,128)}, f32[96,32,128]{2,1,0:T(8,128)}, f32[3,256,384]{2,1,0:T(8,128)}) custom-call(s32[32,1,128]{2,1,0:T(1,128)} %get-tuple-element.10.table_hbm, f32[12,32,16,128]{3,2,1,0:T(8,128)} %get-tuple-element.11.recv0_hbm, f32[12,32,16,128]{3,2,1,0:T(8,128)} %get-tuple-element.12.recv1_hbm, ...), custom_call_target="tpu_custom_call" | custom-call | tf_op jit(solution)/shard_map/assemble/pallas_call | solution.py:531
